TPU v7x, 32 devices: a whole 2x2x4 slice. The times are simulated.
32 devices in a mesh: img: 8 (over y, x, core), atom: 4 (over z).
Axes of the slice: x: 2, y: 2, z: 4, core: 2. Of those that a mesh axis runs over, the one named last changes fastest.
Arguments:
- positions: float32 [3, 256, 4096], P(None, 'img', 'atom'), may hold values from -6 to 6
- strength: float32 [4096], replicated, may hold values from 0.5 to 2
- tile_pairs: int32 [32, 8], replicated, may hold values from 0 to 31
- source_segment: int32 [256], P('img'), may hold values from 1 to 255, as said below
Outputs:
- string: float32 [3, 256, 4096], P(None, 'img', 'atom')
Inputs may be any that keep to these rules, and one draw needn't show every extreme that they name: source_segment[j] is j or j + 1, never 0 and never above 255.
All inputs are finite; a program needn't handle non-finite values.
Results may differ from a plain program's by a relative error of at most 0.0003.
Values sent between devices are 32-bit elements; how exact they have to be, the bound alone decides.
No kernel may reach another device: no remote copies, remote signals or barrier semaphores. Data moves between devices by JAX's collectives and lax.ppermute only.
A program may use at most 64 MiB of HBM per device.

v0:
```python
import jax
import jax.numpy as jnp
from jax import lax
from jax.sharding import PartitionSpec as P

TB = 128


STEP_SIZE = 0.02


def padded(cells, sides, width):
    for axis, dim in sides:
        count = lax.axis_size(axis)
        ends = count - 1
        head = lax.slice_in_dim(cells, 0, width, axis=dim)
        tail = lax.slice_in_dim(cells, cells.shape[dim] - width, cells.shape[dim], axis=dim)
        cells = jnp.concatenate(
            [
                lax.ppermute(tail, axis, [(i, (i + 1) % count) for i in range(ends)]),
                cells,
                lax.ppermute(head, axis, [((i + 1) % count, i) for i in range(ends)]),
            ],
            axis=dim,
        )
    return cells


def pair_force(block_pos, block_strength, whole_pos, strength, partners):
    force_sum = jnp.zeros(block_pos.shape, jnp.float32)
    for neighbor_slot in range(partners.shape[0]):
        first_atom = partners[neighbor_slot] * TB
        partner_pos = lax.dynamic_slice_in_dim(whole_pos, first_atom, TB, 2)
        partner_strength = lax.dynamic_slice_in_dim(strength, first_atom, TB, 0)
        differ = block_pos[:, :, :, None] - partner_pos[:, :, None, :]
        radius = jnp.sum(differ * differ, axis=0)
        coupling = (
            block_strength[None, :, None] * partner_strength[None, None, :] * jnp.exp(-0.5 * radius)
        )
        force_sum = force_sum + jnp.sum(differ * coupling[None], axis=3)
    return force_sum


def block_forces(blocks, indices, strength, tile_pairs, whole_pos):

    def one_block(inputs):
        block_pos, index = inputs
        partners = tile_pairs[index]
        block_strength = lax.dynamic_slice_in_dim(strength, index * TB, TB, 0)
        return pair_force(block_pos, block_strength, whole_pos, strength, partners)

    result = lax.map(one_block, (blocks, indices))
    block_count, _, image_count, _ = result.shape
    return result.transpose(1, 2, 0, 3).reshape(3, image_count, block_count * TB)


def shards(positions, strength, tile_pairs, source_segment):
    count = positions.shape[1]
    local_atoms = positions.shape[2]
    whole_pos = lax.all_gather(positions, "atom", axis=2, tiled=True)
    per_device = local_atoms // TB
    blocks = positions.reshape(3, count, per_device, TB).transpose(2, 0, 1, 3)
    indices = lax.axis_index("atom") * per_device + jnp.arange(per_device, dtype=jnp.int32)
    forces = block_forces(blocks, indices, strength, tile_pairs, whole_pos)
    moved = positions + STEP_SIZE * forces
    first_image = lax.axis_index("img") * count
    images_total = count * lax.axis_size("img")
    extended = padded(moved, (("img", 1),), 1)
    segments = extended[:, 1:] - extended[:, :-1]
    partial_value = jnp.sum(segments * segments, axis=(0, 2))
    squares = lax.psum(partial_value, "atom")
    global_ids = first_image + jnp.arange(count + 1, dtype=jnp.int32)
    valid = (global_ids >= 1) & (global_ids <= images_total - 1)
    lengths = jnp.where(valid, jnp.sqrt(1.0 + squares), jnp.zeros_like(squares))
    running = jnp.cumsum(lengths[:count])
    device_total = running[-1]
    totals = lax.all_gather(device_total[None], "img", axis=0, tiled=True)
    ranks = jnp.arange(totals.shape[0], dtype=jnp.int32)
    offset = jnp.sum(jnp.where(ranks < lax.axis_index("img"), totals, jnp.zeros_like(totals)))
    total_arc = jnp.sum(totals)
    arc_ext = jnp.concatenate(
        [offset[None], offset + running, (offset + device_total + lengths[count])[None]]
    )
    length_ext = jnp.concatenate([jnp.zeros((1,), jnp.float32), lengths])
    upper = source_segment - first_image + 1
    lower = upper - 1
    columns = jnp.arange(count + 2, dtype=jnp.int32)
    hit_low = (columns[None, :] == lower[:, None]).astype(jnp.float32)
    hit_high = (columns[None, :] == upper[:, None]).astype(jnp.float32)
    arc_low = jnp.sum(hit_low * arc_ext[None, :], axis=1)
    seg_length = jnp.sum(hit_high * length_ext[None, :], axis=1)
    target = (first_image + jnp.arange(count, dtype=jnp.int32)).astype(jnp.float32) * (
        total_arc / (images_total - 1)
    )
    weight = (target - arc_low) / seg_length
    mixing = (1.0 - weight)[:, None] * hit_low + weight[:, None] * hit_high
    string = jnp.einsum("je,cea->cja", mixing, extended, precision=lax.Precision.HIGHEST)
    return string


def solution(mesh):
    placed = (P(None, "img", "atom"), P(), P(), P("img"))
    return jax.shard_map(
        shards, mesh=mesh, in_specs=placed, out_specs=P(None, "img", "atom"), check_vma=False
    )
```

profile of v0, /device:TPU:4, one launch (start us, length us, event | category | flops | bytes accessed | tf_op | source)
XLA Modules:
  0.0 445.6 jit_solution(13500189040580754193)
XLA Ops:
  7.3 1.1 copy.15
  8.4 38.8 %all-gather.3.cloned.1.call-done = f32[3,32,4096]{2,1,0:T(8,128)} async-done(((f32[3,32,1024]{2,1,0:T(8,128)}), f32[3,32,4096]{2,1,0:T(8,128)}) %all-gather.3.cloned.1.call-update) | async-done | bytes 1572880 | tf_op jit(solution)/shard_map/all_gather | solution.py:60
  47.2 351.5 %while.10 = (s32[]{:T(128)}, f32[8,3,32,128]{3,2,1,0:T(8,128)}, f32[8,3,32,128]{3,0,2,1:T(8,128)S(1)}, s32[8]{0:T(128)S(1)}, s32[32,8]{0,1:T(8,128)}, /*index=5*...) while((s32[]{:T(128)}, f32[8,3,32,128]{3,2,1,0:T(8,128)}, ...), condition=%wide.region_17.18_spmd, body=%wide.region_0.17_spmd.sunk | while | flops 79810600 | bytes 70826768 | solution.py:52
  49.4 0.8 constant_dynamic-slice_fusion.13
  55.8 1.0 constant_dynamic-slice_fusion.14
  56.9 3.7 fusion.45
  61.2 0.9 fusion.46
  62.2 2.1 exponential_multiply_fusion.15
  64.4 10.2 %fusion.47 = (f32[3,32,128]{2,1,0:T(8,128)S(1)}, f32[32,128,128]{2,1,0:T(8,128)S(1)}, f32[32,128,128]{2,1,0:T(8,128)S(1)}, f32[32,128,128]{2,1,0:T(8,128)S(1)}, ...) fusion(f32[32,128,128]{2,1,0:T(8,128)S(1)} %get-tuple-element.2, ...), kind=kLoop, calls=%fused_computation.19.clone.1 | loop fusion | flops 34578432 | bytes 17317888 | tf_op jit(solution)/shard_map/while/body/eval_jaxpr/reduce_sum | solution.py:40
  76.3 14.1 %fusion.48 = (f32[3,32,128]{2,1,0:T(8,128)S(1)}, f32[3,32,128]{2,1,0:T(8,128)S(1)}, f32[3,32,128]{2,1,0:T(8,128)S(1)}, f32[3,32,128]{2,1,0:T(8,128)S(1)}, f32[3,...) fusion(f32[32,128,128]{2,1,0:T(8,128)S(1)} %exponential_multiply_fusion.16, ...), kind=kLoop, calls=%fused_computation.21.clone.1 | loop fusion | flops 28237824 | bytes 13221888 | tf_op jit(solution)/shard_map/while/body/eval_jaxpr/reduce_sum | solution.py:40
  99.8 1.0 constant_dynamic-slice_fusion.14
  100.8 3.7 fusion.45
  105.1 0.9 fusion.46
  106.1 2.1 exponential_multiply_fusion.15
  108.3 10.2 %fusion.47 = (f32[3,32,128]{2,1,0:T(8,128)S(1)}, f32[32,128,128]{2,1,0:T(8,128)S(1)}, f32[32,128,128]{2,1,0:T(8,128)S(1)}, f32[32,128,128]{2,1,0:T(8,128)S(1)}, ...) fusion(f32[32,128,128]{2,1,0:T(8,128)S(1)} %get-tuple-element.2, ...), kind=kLoop, calls=%fused_computation.19.clone.1 | loop fusion | flops 34578432 | bytes 17317888 | tf_op jit(solution)/shard_map/while/body/eval_jaxpr/reduce_sum | solution.py:40
  120.2 14.1 %fusion.48 = (f32[3,32,128]{2,1,0:T(8,128)S(1)}, f32[3,32,128]{2,1,0:T(8,128)S(1)}, f32[3,32,128]{2,1,0:T(8,128)S(1)}, f32[3,32,128]{2,1,0:T(8,128)S(1)}, f32[3,...) fusion(f32[32,128,128]{2,1,0:T(8,128)S(1)} %exponential_multiply_fusion.16, ...), kind=kLoop, calls=%fused_computation.21.clone.1 | loop fusion | flops 28237824 | bytes 13221888 | tf_op jit(solution)/shard_map/while/body/eval_jaxpr/reduce_sum | solution.py:40
  137.3 0.8 constant_dynamic-slice_fusion.13
  143.7 1.0 constant_dynamic-slice_fusion.14
  144.8 3.7 fusion.45
  149.0 1.0 fusion.46
  150.1 2.1 exponential_multiply_fusion.15
  152.2 10.2 %fusion.47 = (f32[3,32,128]{2,1,0:T(8,128)S(1)}, f32[32,128,128]{2,1,0:T(8,128)S(1)}, f32[32,128,128]{2,1,0:T(8,128)S(1)}, f32[32,128,128]{2,1,0:T(8,128)S(1)}, ...) fusion(f32[32,128,128]{2,1,0:T(8,128)S(1)} %get-tuple-element.2, ...), kind=kLoop, calls=%fused_computation.19.clone.1 | loop fusion | flops 34578432 | bytes 17317888 | tf_op jit(solution)/shard_map/while/body/eval_jaxpr/reduce_sum | solution.py:40
  164.1 14.1 %fusion.48 = (f32[3,32,128]{2,1,0:T(8,128)S(1)}, f32[3,32,128]{2,1,0:T(8,128)S(1)}, f32[3,32,128]{2,1,0:T(8,128)S(1)}, f32[3,32,128]{2,1,0:T(8,128)S(1)}, f32[3,...) fusion(f32[32,128,128]{2,1,0:T(8,128)S(1)} %exponential_multiply_fusion.16, ...), kind=kLoop, calls=%fused_computation.21.clone.1 | loop fusion | flops 28237824 | bytes 13221888 | tf_op jit(solution)/shard_map/while/body/eval_jaxpr/reduce_sum | solution.py:40
  187.6 1.0 constant_dynamic-slice_fusion.14
  188.7 3.7 fusion.45
  192.9 1.0 fusion.46
  194.0 2.1 exponential_multiply_fusion.15
  196.2 10.2 %fusion.47 = (f32[3,32,128]{2,1,0:T(8,128)S(1)}, f32[32,128,128]{2,1,0:T(8,128)S(1)}, f32[32,128,128]{2,1,0:T(8,128)S(1)}, f32[32,128,128]{2,1,0:T(8,128)S(1)}, ...) fusion(f32[32,128,128]{2,1,0:T(8,128)S(1)} %get-tuple-element.2, ...), kind=kLoop, calls=%fused_computation.19.clone.1 | loop fusion | flops 34578432 | bytes 17317888 | tf_op jit(solution)/shard_map/while/body/eval_jaxpr/reduce_sum | solution.py:40
  208.1 14.1 %fusion.48 = (f32[3,32,128]{2,1,0:T(8,128)S(1)}, f32[3,32,128]{2,1,0:T(8,128)S(1)}, f32[3,32,128]{2,1,0:T(8,128)S(1)}, f32[3,32,128]{2,1,0:T(8,128)S(1)}, f32[3,...) fusion(f32[32,128,128]{2,1,0:T(8,128)S(1)} %exponential_multiply_fusion.16, ...), kind=kLoop, calls=%fused_computation.21.clone.1 | loop fusion | flops 28237824 | bytes 13221888 | tf_op jit(solution)/shard_map/while/body/eval_jaxpr/reduce_sum | solution.py:40
  225.2 0.8 constant_dynamic-slice_fusion.13
  231.6 1.0 constant_dynamic-slice_fusion.14
  232.7 3.7 fusion.45
  236.9 1.0 fusion.46
  238.0 2.1 exponential_multiply_fusion.15
  240.1 10.2 %fusion.47 = (f32[3,32,128]{2,1,0:T(8,128)S(1)}, f32[32,128,128]{2,1,0:T(8,128)S(1)}, f32[32,128,128]{2,1,0:T(8,128)S(1)}, f32[32,128,128]{2,1,0:T(8,128)S(1)}, ...) fusion(f32[32,128,128]{2,1,0:T(8,128)S(1)} %get-tuple-element.2, ...), kind=kLoop, calls=%fused_computation.19.clone.1 | loop fusion | flops 34578432 | bytes 17317888 | tf_op jit(solution)/shard_map/while/body/eval_jaxpr/reduce_sum | solution.py:40
  252.1 14.1 %fusion.48 = (f32[3,32,128]{2,1,0:T(8,128)S(1)}, f32[3,32,128]{2,1,0:T(8,128)S(1)}, f32[3,32,128]{2,1,0:T(8,128)S(1)}, f32[3,32,128]{2,1,0:T(8,128)S(1)}, f32[3,...) fusion(f32[32,128,128]{2,1,0:T(8,128)S(1)} %exponential_multiply_fusion.16, ...), kind=kLoop, calls=%fused_computation.21.clone.1 | loop fusion | flops 28237824 | bytes 13221888 | tf_op jit(solution)/shard_map/while/body/eval_jaxpr/reduce_sum | solution.py:40
  275.5 1.0 constant_dynamic-slice_fusion.14
  276.6 3.7 fusion.45
  280.9 0.9 fusion.46
  281.9 2.1 exponential_multiply_fusion.15
  284.1 10.2 %fusion.47 = (f32[3,32,128]{2,1,0:T(8,128)S(1)}, f32[32,128,128]{2,1,0:T(8,128)S(1)}, f32[32,128,128]{2,1,0:T(8,128)S(1)}, f32[32,128,128]{2,1,0:T(8,128)S(1)}, ...) fusion(f32[32,128,128]{2,1,0:T(8,128)S(1)} %get-tuple-element.2, ...), kind=kLoop, calls=%fused_computation.19.clone.1 | loop fusion | flops 34578432 | bytes 17317888 | tf_op jit(solution)/shard_map/while/body/eval_jaxpr/reduce_sum | solution.py:40
  296.0 14.1 %fusion.48 = (f32[3,32,128]{2,1,0:T(8,128)S(1)}, f32[3,32,128]{2,1,0:T(8,128)S(1)}, f32[3,32,128]{2,1,0:T(8,128)S(1)}, f32[3,32,128]{2,1,0:T(8,128)S(1)}, f32[3,...) fusion(f32[32,128,128]{2,1,0:T(8,128)S(1)} %exponential_multiply_fusion.16, ...), kind=kLoop, calls=%fused_computation.21.clone.1 | loop fusion | flops 28237824 | bytes 13221888 | tf_op jit(solution)/shard_map/while/body/eval_jaxpr/reduce_sum | solution.py:40
  313.0 0.8 constant_dynamic-slice_fusion.13
  319.5 1.0 constant_dynamic-slice_fusion.14
  320.5 3.7 fusion.45
  324.8 1.0 fusion.46
  325.9 2.1 exponential_multiply_fusion.15
  328.0 10.2 %fusion.47 = (f32[3,32,128]{2,1,0:T(8,128)S(1)}, f32[32,128,128]{2,1,0:T(8,128)S(1)}, f32[32,128,128]{2,1,0:T(8,128)S(1)}, f32[32,128,128]{2,1,0:T(8,128)S(1)}, ...) fusion(f32[32,128,128]{2,1,0:T(8,128)S(1)} %get-tuple-element.2, ...), kind=kLoop, calls=%fused_computation.19.clone.1 | loop fusion | flops 34578432 | bytes 17317888 | tf_op jit(solution)/shard_map/while/body/eval_jaxpr/reduce_sum | solution.py:40
  339.9 14.1 %fusion.48 = (f32[3,32,128]{2,1,0:T(8,128)S(1)}, f32[3,32,128]{2,1,0:T(8,128)S(1)}, f32[3,32,128]{2,1,0:T(8,128)S(1)}, f32[3,32,128]{2,1,0:T(8,128)S(1)}, f32[3,...) fusion(f32[32,128,128]{2,1,0:T(8,128)S(1)} %exponential_multiply_fusion.16, ...), kind=kLoop, calls=%fused_computation.21.clone.1 | loop fusion | flops 28237824 | bytes 13221888 | tf_op jit(solution)/shard_map/while/body/eval_jaxpr/reduce_sum | solution.py:40
  363.4 1.0 constant_dynamic-slice_fusion.14
  364.5 3.7 fusion.45
  368.7 0.9 fusion.46
  369.8 2.1 exponential_multiply_fusion.15
  371.9 10.2 %fusion.47 = (f32[3,32,128]{2,1,0:T(8,128)S(1)}, f32[32,128,128]{2,1,0:T(8,128)S(1)}, f32[32,128,128]{2,1,0:T(8,128)S(1)}, f32[32,128,128]{2,1,0:T(8,128)S(1)}, ...) fusion(f32[32,128,128]{2,1,0:T(8,128)S(1)} %get-tuple-element.2, ...), kind=kLoop, calls=%fused_computation.19.clone.1 | loop fusion | flops 34578432 | bytes 17317888 | tf_op jit(solution)/shard_map/while/body/eval_jaxpr/reduce_sum | solution.py:40
  383.9 14.1 %fusion.48 = (f32[3,32,128]{2,1,0:T(8,128)S(1)}, f32[3,32,128]{2,1,0:T(8,128)S(1)}, f32[3,32,128]{2,1,0:T(8,128)S(1)}, f32[3,32,128]{2,1,0:T(8,128)S(1)}, f32[3,...) fusion(f32[32,128,128]{2,1,0:T(8,128)S(1)} %exponential_multiply_fusion.16, ...), kind=kLoop, calls=%fused_computation.21.clone.1 | loop fusion | flops 28237824 | bytes 13221888 | tf_op jit(solution)/shard_map/while/body/eval_jaxpr/reduce_sum | solution.py:40
  398.7 1.0 bitcast_add_fusion
  399.7 1.9 collective-permute-start
  401.7 4.5 %collective-permute-start.1 = (f32[3,1,1024]{2,1,0:T(1,128)S(1)}, f32[3,1,1024]{2,1,0:T(1,128)S(1)}, u32[]{:S(2)}, u32[]{:S(2)}) collective-permute-start(f32[3,1,1024]{2,1,0:T(1,128)S(1)} %get-tuple-element.129), channel_id=1, source_target_pairs={{4,0},{8,4},{12,8},{16,12},{20,16},{24,20},{28,24},{5,1},{9,5},{13... | collective-permute-start | bytes 36872 | tf_op jit(solution)/shard_map/ppermute | solution.py:22
  407.8 9.6 %psum.7 = f32[33]{0:T(128)S(1)} all-reduce(f32[33]{0:T(128)S(1)} %fusion.22), channel_id=1, replica_groups=mesh['img'=8,'atom'=4] {'atom'}, use_global_device_ids=true, to_apply=%region_19.20 | all-reduce | flops 33 | bytes 264 | tf_op jit(solution)/shard_map/psum | solution.py:71
  418.1 1.3 bitcast_dynamic-update-slice_fusion.1
  420.0 12.4 %all-reduce = f32[8]{0:T(128)S(1)} all-reduce(f32[8]{0:T(128)S(1)} %bitcast_dynamic-update-slice_fusion.1), channel_id=2, replica_groups=mesh['img'=8,'atom'=4] {'img'}, use_global_device_ids=true, to_apply=%add | all-reduce | flops 8 | bytes 64 | tf_op jit(solution)/shard_map/all_gather | solution.py:77
  433.0 0.8 add_reduce_fusion
  436.4 0.8 pad_maximum_fusion
  437.4 1.3 convolution_bitcast_fusion
  (120 shorter events, 37.3 us)
Async XLA Ops:
  6.5 40.6 %all-gather.3.cloned.1.call-start = ((), (), s32[]{:S(2)}) async-start(), calls=%async_computation | async-start | bytes 1966080 | tf_op jit(solution)/shard_map/all_gather | solution.py:60
  47.2 351.5 %copy-start = (f32[3,32,1024]{2,1,0:T(8,128)S(1)}, f32[3,32,1024]{2,1,0:T(8,128)}, u32[]{:S(2)}) copy-start(f32[3,32,1024]{2,1,0:T(8,128)} %param.6) | copy-start | bytes 1179652
  47.2 359.1 %copy-start.1 = (s32[32]{0:T(128)S(1)}, s32[32]{0:T(128)}, u32[]{:S(2)}) copy-start(s32[32]{0:T(128)} %param.9) | copy-start | bytes 388
  47.2 359.1 %copy-start.2 = (u32[32]{0:T(128)S(1)}, u32[32]{0:T(128)}, u32[]{:S(2)}) copy-start(u32[32]{0:T(128)} %constant.75) | copy-start | bytes 388
  399.7 7.1 %collective-permute-start = (f32[3,1,1024]{2,1,0:T(1,128)S(1)}, f32[3,1,1024]{2,1,0:T(1,128)S(1)}, u32[]{:S(2)}, u32[]{:S(2)}) collective-permute-start(f32[3,1,1024]{2,1,0:T(1,128)S(1)} %get-tuple-element.128), channel_id=1, source_target_pairs={{0,4},{4,8},{8,12},{12,16},{16,20},{20,24},{24,28},{1,5},{5,9},{9,... | collective-permute-start | bytes 36872 | tf_op jit(solution)/shard_map/ppermute | solution.py:20
  401.7 5.9 %collective-permute-start.1 = (f32[3,1,1024]{2,1,0:T(1,128)S(1)}, f32[3,1,1024]{2,1,0:T(1,128)S(1)}, u32[]{:S(2)}, u32[]{:S(2)}) collective-permute-start(f32[3,1,1024]{2,1,0:T(1,128)S(1)} %get-tuple-element.129), channel_id=1, source_target_pairs={{4,0},{8,4},{12,8},{16,12},{20,16},{24,20},{28,24},{5,1},{9,5},{13... | collective-permute-start | bytes 36872 | tf_op jit(solution)/shard_map/ppermute | solution.py:22
Sparse Core Ops, SparseCore 0:
  8.9 38.2 all-gather.2
where the time goes:
time: 448 us; the launch traced here: 446 us
  other arithmetic  264 us (59%)
  loops' own time  58.9 us (13%)
  waiting for transfers between devices  40.2 us (9%)
  local copies, waits for them, and re-layouts  36.2 us (8%)
  blocking collectives  21.9 us (5%)
  between operations  16.1 us (4%)
  starting transfers between devices  6.46 us (1%)
    reduce_sum x16, other arithmetic, pair_force(): force_sum = force_sum + jnp.sum(differ * coupling[None], axis=3)  194 us
    another operation x1, loops' own time, block_forces(): result = lax.map(one_block, (blocks, indices))  58.9 us
    all_gather x1, waiting for transfers between devices, shards(): whole_pos = lax.all_gather(positions, 'atom', axis=2, tiled=True)  38.8 us
    mul x64, other arithmetic, pair_force(): block_strength[None, :, None] * partner_strength[None, None, :]  31.5 us
    reduce_sum x8, other arithmetic, pair_force(): radius = jnp.sum(differ * differ, axis=0)  29.4 us
    all_gather x1, blocking collectives, shards(): totals = lax.all_gather(device_total[None], 'img', axis=0, tiled=True)  12.4 us
    psum x1, blocking collectives, shards(): squares = lax.psum(partial_value, 'atom')  9.57 us
  transfers between devices with their start and end apart: 3, of which 2 were waited for; matrix products, arithmetic and copies ran while one was open for 0% of the time, Pallas kernels for 0%

commit v1 on v0

v1 whole, which is shorter than its diff:
```python
import jax
import jax.numpy as jnp
from jax import lax
from jax.experimental import pallas as pl
from jax.experimental.pallas import tpu as pltpu
from jax.sharding import PartitionSpec as P

TB = 128
ROWS = 8
FEATURE_BLOCKS = 7
DEPTH = 128
LOG2E = 1.4426950408889634
STEP_SIZE = 0.02


def three_parts(value):
    high = value.astype(jnp.bfloat16).astype(jnp.float32)
    rest = value - high
    middle = rest.astype(jnp.bfloat16).astype(jnp.float32)
    return high, middle, rest - middle


def force_kernel(pairs_ref, x_ref, strength_ref, out_ref, partner_ref, own_ref, sum_ref):
    images, _, atoms = x_ref.shape
    tiles = atoms // TB
    row = lax.broadcasted_iota(jnp.int32, (ROWS, atoms), 0)
    one = jnp.ones((ROWS, atoms), jnp.float32)
    zero = jnp.zeros((ROWS, atoms), jnp.float32)
    log_strength = jnp.log(strength_ref[...]) * LOG2E
    for pair in range(images // 2):
        partner_rows = []
        for side in range(2):
            x = x_ref[2 * pair + side]
            xh, xm, xl = three_parts(x)
            vh, vm, vl = three_parts(x * LOG2E)
            const = (-0.5 * LOG2E) * jnp.sum(x * x, axis=0, keepdims=True) + log_strength
            ch, cm, cl = three_parts(jnp.broadcast_to(const, (ROWS, atoms)))
            first = jnp.where(row == 0, ch, jnp.where(row == 1, cm, cl))
            c_partner = jnp.where(row < 3, first, jnp.where(row < 6, one, zero))
            second = jnp.where(row == 3, ch, jnp.where(row == 4, cm, cl))
            c_own = jnp.where(row < 3, one, jnp.where(row < 6, second, zero))
            partner_rows += [xh, xh, xm, xm, xh, xl, c_partner]
            own = [vh, vm, vh, vm, vl, vh, c_own]
            blank = [zero] * FEATURE_BLOCKS
            own = (own + blank if side == 0 else blank + own) + [zero] * (
                DEPTH // ROWS - 2 * FEATURE_BLOCKS
            )
            own = jnp.concatenate(own, axis=0).astype(jnp.bfloat16)
            tops = jnp.where(row == 3, one, xh)
            parts = jnp.concatenate([tops, xm, xl], axis=0).astype(jnp.bfloat16)
            for tile in range(tiles):
                cut = slice(tile * TB, (tile + 1) * TB)
                own_ref[pair, tile, :, side * TB : (side + 1) * TB] = own[:, cut]
                for half in range(2):
                    sum_ref[pair, tile, 24 * side : 24 * side + 24, half * TB : (half + 1) * TB] = (
                        parts[:, cut]
                    )
        partner_rows += [zero] * (DEPTH // ROWS - 2 * FEATURE_BLOCKS)
        partner = jnp.concatenate(partner_rows, axis=0)
        for tile in range(tiles):
            partner_ref[pair, tile] = partner[:, tile * TB : (tile + 1) * TB].T.astype(jnp.bfloat16)

    slots = pairs_ref.shape[1]

    def step(index, carry):
        pair = index // tiles
        tile = index % tiles
        own = own_ref[pair, tile]
        acc = jnp.zeros((48, 2 * TB), jnp.float32)
        for slot in range(slots):
            other = pairs_ref[tile, slot]
            power = jnp.dot(partner_ref[pair, other], own, preferred_element_type=jnp.float32)
            w = jnp.exp2(power)
            high = w.astype(jnp.bfloat16)
            low = (w - high.astype(jnp.float32)).astype(jnp.bfloat16)
            both = jnp.concatenate([high, low], axis=0)
            acc = acc + jnp.dot(sum_ref[pair, other], both, preferred_element_type=jnp.float32)
        lanes = pl.ds(pl.multiple_of(tile * TB, TB), TB)
        for side in range(2):
            part = acc[24 * side : 24 * side + 24, side * TB : (side + 1) * TB]
            total = part[0:8] + part[8:16] + part[16:24]
            x = x_ref[2 * pair + side, :, lanes]
            force = x * total[3:4] - total
            out_ref[2 * pair + side, :, lanes] = x + STEP_SIZE * force
        return carry

    lax.fori_loop(0, (images // 2) * tiles, step, 0)


def moved_images(x, strength, tile_pairs):
    images, _, atoms = x.shape
    tiles = atoms // TB
    pairs = images // 2
    vmem = pl.BlockSpec(memory_space=pltpu.VMEM)
    return pl.pallas_call(
        force_kernel,
        out_shape=jax.ShapeDtypeStruct(x.shape, jnp.float32),
        in_specs=[pl.BlockSpec(memory_space=pltpu.SMEM), vmem, vmem],
        out_specs=vmem,
        scratch_shapes=[
            pltpu.VMEM((pairs, tiles, TB, DEPTH), jnp.bfloat16),
            pltpu.VMEM((pairs, tiles, DEPTH, 2 * TB), jnp.bfloat16),
            pltpu.VMEM((pairs, tiles, 48, 2 * TB), jnp.bfloat16),
        ],
        name="force",
    )(tile_pairs, x, strength[None, :])


def shards(positions, strength, tile_pairs, source_segment):
    count = positions.shape[1]
    blocks = lax.axis_size("atom")
    mine = count // blocks
    images_total = count * lax.axis_size("img")
    own = lax.all_to_all(positions, "atom", split_axis=1, concat_axis=2, tiled=True)
    x = jnp.pad(own.transpose(1, 0, 2), ((0, 0), (0, ROWS - 3), (0, 0)))
    moved = moved_images(x, strength, tile_pairs)[:, :3]
    everyone = images_total // mine
    before = lax.ppermute(
        moved[mine - 1 :], ("img", "atom"), [(i, i + 1) for i in range(everyone - 1)]
    )
    segments = moved - jnp.concatenate([before, moved[: mine - 1]], axis=0)
    squares = jnp.sum(segments * segments, axis=(1, 2))
    first = lax.axis_index(("img", "atom")) * mine
    ids = first + jnp.arange(mine, dtype=jnp.int32)
    own_lengths = jnp.where(ids >= 1, jnp.sqrt(1.0 + squares), 0.0)
    lengths = lax.all_gather(own_lengths, ("img", "atom"), axis=0, tiled=True)
    back = lax.all_to_all(moved.transpose(1, 0, 2), "atom", split_axis=2, concat_axis=1, tiled=True)
    ends = lax.axis_size("img") - 1
    head = lax.ppermute(back[:, count - 1 :], "img", [(i, i + 1) for i in range(ends)])
    tail = lax.ppermute(back[:, :1], "img", [(i + 1, i) for i in range(ends)])
    numbers = lax.axis_index("img") * count + jnp.arange(count, dtype=jnp.int32)
    columns = jnp.arange(images_total, dtype=jnp.int32)[None, :]
    segment = source_segment[:, None]
    arc_low = jnp.sum(jnp.where(columns < segment, lengths[None, :], 0.0), axis=1)
    span = jnp.sum(jnp.where(columns == segment, lengths[None, :], 0.0), axis=1)
    target = numbers.astype(jnp.float32) * (jnp.sum(lengths) / (images_total - 1))
    weight = ((target - arc_low) / span)[None, :, None]
    later = (source_segment > numbers)[None, :, None]
    previous = jnp.concatenate([head, back[:, : count - 1]], axis=1)
    following = jnp.concatenate([back[:, 1:], tail], axis=1)
    low = jnp.where(later, back, previous)
    high = jnp.where(later, following, back)
    return (1.0 - weight) * low + weight * high


def solution(mesh):
    placed = (P(None, "img", "atom"), P(), P(), P("img"))
    return jax.shard_map(
        shards, mesh=mesh, in_specs=placed, out_specs=P(None, "img", "atom"), check_vma=False
    )
```

time: 448 us -> 198 us (0.44)
  other arithmetic: 264 us -> 5.17 us
  Pallas kernels: 0 us -> 75.4 us
  loops' own time: 58.9 us -> 0 us
  waiting for transfers between devices: 40.2 us -> 20.4 us
  blocking collectives: 21.9 us -> 40.7 us
  between operations: 16.1 us -> 0.85 us
  starting transfers between devices: 6.46 us -> 16.7 us
    reduce_sum x27 -> x3, other arithmetic: 225 us -> 2.39 us  [the longest x1 1.53 us: shards(): squares = jnp.sum(segments * segments, axis=(1, 2))]
    pallas_call x0 -> x1, Pallas kernels: none -> 75.4 us  [moved_images(): pl.pallas_call(force_kernel, out_shape=jax.ShapeDtypeStruct(x.shape, jnp....]
    another operation x1 -> x0, loops' own time: 58.9 us -> none  [block_forces(): result = lax.map(one_block, (blocks, indices))]
    unnamed x0 -> x1, blocking collectives: none -> 40.7 us
    all_gather x1 -> x0, waiting for transfers between devices: 38.8 us -> none  [shards(): whole_pos = lax.all_gather(positions, 'atom', axis=2, tiled=True)]
    mul x64 -> x0, other arithmetic: 31.5 us -> none  [pair_force(): block_strength[None, :, None] * partner_strength[None, None, :]]
    dynamic_slice x40 -> x0, local copies, waits for them, and re-layouts: 27 us -> none  [the longest x8 8.16 us: pair_force(): partner_pos = lax.dynamic_slice_in_dim(whole_pos, first_atom, TB, 2)]
    unnamed x10 -> x7, local copies, waits for them, and re-layouts: 2.97 us -> 19.6 us
  transfers between devices with their start and end apart: 3 -> 5, of which waited for: 2 -> 3; matrix products, arithmetic and copies ran while one was open for 0% -> 2% of each run, Pallas kernels for 0% -> 0%
where the time goes in v1:
time: 198 us; the launch traced here: 196 us
  Pallas kernels  75.4 us (38%)
  blocking collectives  40.7 us (21%)
  local copies, waits for them, and re-layouts  36.4 us (18%)
  waiting for transfers between devices  20.4 us (10%)
  starting transfers between devices  16.7 us (8%)
  other arithmetic  5.17 us (3%)
    pallas_call x1, Pallas kernels, moved_images(): pl.pallas_call(force_kernel, out_shape=jax.ShapeDtypeStruct(x.shape, jnp....  75.4 us
    unnamed x1, blocking collectives  40.7 us
    unnamed x7, local copies, waits for them, and re-layouts  19.6 us
    all_to_all x1, waiting for transfers between devices, shards(): lax.all_to_all(positions, 'atom', split_axis=1, concat_axis=2, tiled=True)  13.1 us
    all_to_all x2, local copies, waits for them, and re-layouts, shards(): lax.all_to_all(moved.transpose(1, 0, 2), 'atom', split_axis=2, concat_axi...  6.89 us
    ppermute x1, waiting for transfers between devices, shards(): lax.ppermute(moved[mine - 1:], ('img', 'atom'), [(i, i + 1) for i in rang...  6 us
    transpose x1, local copies, waits for them, and re-layouts, shards(): moved.transpose(1, 0, 2)  5.81 us
    all_to_all x1, starting transfers between devices, shards(): lax.all_to_all(positions, 'atom', split_axis=1, concat_axis=2, tiled=True)  4.87 us
  transfers between devices with their start and end apart: 5, of which 3 were waited for; matrix products, arithmetic and copies ran while one was open for 2% of the time, Pallas kernels for 0%

profile of v1, /device:TPU:4, one launch (start us, length us, event | category | flops | bytes accessed | tf_op | source)
XLA Modules:
  0.0 195.7 jit_solution(6792136006590383652)
XLA Ops:
  0.0 2.1 %copy.31 = f32[3,32,1024]{2,0,1:T(4,128)} copy(f32[3,32,1024]{2,1,0:T(8,128)} %param.4) | data formatting | bytes 786432 | tf_op args[0]
  2.1 4.9 %all-to-all-start = ((f32[3,32,1024]{2,0,1:T(4,128)}), f32[3,32,1024]{2,0,1:T(4,128)S(1)}, u32[]{:S(2)}, u32[]{:S(2)}) async-start(f32[3,32,1024]{2,0,1:T(4,128)} %copy.31), calls=%async_computation | async-start | bytes 1048576 | tf_op jit(solution)/shard_map/all_to_all | solution.py:114
  6.9 1.4 copy.34.pairs_ref
  8.3 13.1 %all-to-all-done = f32[3,32,1024]{2,0,1:T(4,128)S(1)} async-done(((f32[3,32,1024]{2,0,1:T(4,128)}), f32[3,32,1024]{2,0,1:T(4,128)S(1)}, u32[]{:S(2)}, u32[]{:S(2)}) %all-to-all-start) | async-done | bytes 393248 | tf_op jit(solution)/shard_map/all_to_all | solution.py:114
  21.4 0.3 copy.43
  21.7 0.3 all_to_all.29
  22.0 0.3 copy.42
  22.2 1.1 pad.4.x_ref
  23.3 75.4 %force.1 = f32[8,8,4096]{2,1,0:T(8,128)} custom-call(s32[32,8]{1,0:T(8,128)} %copy.34.pairs_ref, f32[8,8,4096]{2,1,0:T(8,128)} %pad.4.x_ref, f32[1,4096]{1,0:T(1,128)} %bitcast.25), custom_call_target="tpu_custom_call" | custom-call | tf_op jit(solution)/shard_map/force/pallas_call | solution.py:95
  98.7 0.9 slice.31
  99.6 1.9 collective-permute-start
  101.5 1.2 slice.32
  102.8 6.0 %collective-permute-done = f32[1,3,4096]{2,1,0:T(4,128)S(1)} collective-permute-done((f32[1,3,4096]{2,1,0:T(4,128)S(1)}, f32[1,3,4096]{2,1,0:T(4,128)S(1)}, u32[]{:S(2)}, u32[]{:S(2)}) %collective-permute-start) | collective-permute-done | bytes 49184 | tf_op jit(solution)/shard_map/ppermute | solution.py:118
  108.8 1.5 fusion.1
  110.3 0.0 copy-start
  110.3 5.8 %copy.35 = f32[3,8,4096]{1,0,2:T(4,128)} copy(f32[3,8,4096]{2,0,1:T(4,128)S(1)} %get-tuple-element.10) | data formatting | bytes 786432 | tf_op jit(solution)/shard_map/transpose | solution.py:127
  116.1 7.5 %reshape.25 = f32[4,1,24576]{2,1,0:T(1,128)} reshape(f32[4096,3,8]{2,1,0:T(4,128)} %bitcast.18) | data formatting | bytes 786432
  123.7 3.5 %all-to-all-start.1 = ((f32[4,1,24576]{2,1,0:T(1,128)}), f32[4,1,24576]{2,1,0:T(1,128)S(1)}, u32[]{:S(2)}, u32[]{:S(2)}) async-start(f32[4,1,24576]{2,1,0:T(1,128)} %reshape.25), calls=%async_computation.1 | async-start | bytes 786432 | tf_op jit(solution)/shard_map/all_to_all | solution.py:127
  127.1 0.0 copy-done
  127.2 0.1 fusion.5
  127.3 40.7 %all-reduce.1 = f32[256]{0:T(256)S(1)} all-reduce(f32[256]{0:T(256)S(1)} %fusion.5), channel_id=1, replica_groups=mesh['img'=8,'atom'=4] {'img','atom'}, use_global_device_ids=true, to_apply=%add.1 | all-reduce | flops 256 | bytes 2048
  168.0 0.7 reduce_sum.37
  169.4 0.2 select_reduce_fusion.1
  169.6 0.0 all-to-all-done.1
  169.6 0.5 broadcast.35
  170.1 1.8 reduce.1
  171.8 8.7 %reshape.26 = f32[4096,3,8]{2,1,0:T(4,128)} reshape(f32[4,24576]{1,0:T(4,128)S(1)} %reduce.1) | data formatting | bytes 786432
  180.5 6.4 %copy.37 = f32[3,4,8,1024]{3,2,1,0:T(8,128)S(1)} copy(f32[3,4,8,1024]{2,0,3,1:T(4,128)} %bitcast.19) | data formatting | bytes 786432 | tf_op jit(solution)/shard_map/all_to_all | solution.py:127
  186.9 1.9 collective-permute-start.1
  188.9 4.5 %collective-permute-start.2 = (f32[3,1,1024]{2,1,0:T(1,128)S(1)}, f32[3,1,1024]{2,1,0:T(1,128)S(1)}, u32[]{:S(2)}, u32[]{:S(2)}) collective-permute-start(f32[3,1,1024]{2,1,0:T(1,128)S(1)} %get-tuple-element.13), channel_id=1, source_target_pairs={{4,0},{8,4},{12,8},{16,12},{20,16},{24,20},{28,24},{5,1},{9,5},{13... | collective-permute-start | bytes 36872 | tf_op jit(solution)/shard_map/ppermute | solution.py:130
  193.4 0.1 fusion.7
  193.5 0.0 collective-permute-done.1
  193.5 1.3 collective-permute-done.2
  194.8 0.9 fusion.3
  (4 shorter events, 0.1 us)
Async XLA Ops:
  2.1 19.4 %all-to-all-start = ((f32[3,32,1024]{2,0,1:T(4,128)}), f32[3,32,1024]{2,0,1:T(4,128)S(1)}, u32[]{:S(2)}, u32[]{:S(2)}) async-start(f32[3,32,1024]{2,0,1:T(4,128)} %copy.31), calls=%async_computation | async-start | bytes 1048576 | tf_op jit(solution)/shard_map/all_to_all | solution.py:114
  99.6 9.2 %collective-permute-start = (f32[1,3,4096]{2,1,0:T(4,128)S(1)}, f32[1,3,4096]{2,1,0:T(4,128)S(1)}, u32[]{:S(2)}, u32[]{:S(2)}) collective-permute-start(f32[1,3,4096]{2,1,0:T(4,128)S(1)} %slice.31), channel_id=1, source_target_pairs={{0,1},{1,2},{2,3},{3,4},{4,5},{5,6},{6,7},{7,8},{8,9},{9,10},{10,1... | collective-permute-start | bytes 147464 | tf_op jit(solution)/shard_map/ppermute | solution.py:118
  110.3 16.8 %copy-start = (s32[32]{0:T(128)S(1)}, s32[32]{0:T(128)}, u32[]{:S(2)}) copy-start(s32[32]{0:T(128)} %param.7) | copy-start | bytes 388
  123.7 45.9 %all-to-all-start.1 = ((f32[4,1,24576]{2,1,0:T(1,128)}), f32[4,1,24576]{2,1,0:T(1,128)S(1)}, u32[]{:S(2)}, u32[]{:S(2)}) async-start(f32[4,1,24576]{2,1,0:T(1,128)} %reshape.25), calls=%async_computation.1 | async-start | bytes 786432 | tf_op jit(solution)/shard_map/all_to_all | solution.py:127
  186.9 6.5 %collective-permute-start.1 = (f32[3,1,1024]{2,1,0:T(1,128)S(1)}, f32[3,1,1024]{2,1,0:T(1,128)S(1)}, u32[]{:S(2)}, u32[]{:S(2)}) collective-permute-start(f32[3,1,1024]{2,1,0:T(1,128)S(1)} %get-tuple-element.14), channel_id=1, source_target_pairs={{0,4},{4,8},{8,12},{12,16},{16,20},{20,24},{24,28},{1,5},{5,9},{9,... | collective-permute-start | bytes 36872 | tf_op jit(solution)/shard_map/ppermute | solution.py:129
  188.9 5.9 %collective-permute-start.2 = (f32[3,1,1024]{2,1,0:T(1,128)S(1)}, f32[3,1,1024]{2,1,0:T(1,128)S(1)}, u32[]{:S(2)}, u32[]{:S(2)}) collective-permute-start(f32[3,1,1024]{2,1,0:T(1,128)S(1)} %get-tuple-element.13), channel_id=1, source_target_pairs={{4,0},{8,4},{12,8},{16,12},{20,16},{24,20},{28,24},{5,1},{9,5},{13... | collective-permute-start | bytes 36872 | tf_op jit(solution)/shard_map/ppermute | solution.py:130

commit v2 on v1

--- a/solution.py
+++ b/solution.py
@@ -11,6 +11,7 @@
 DEPTH = 128
 LOG2E = 1.4426950408889634
 STEP_SIZE = 0.02
+UNROLL = 8
 
 
 def three_parts(value):
@@ -20,8 +21,11 @@
     return high, middle, rest - middle
 
 
-def force_kernel(pairs_ref, x_ref, strength_ref, out_ref, partner_ref, own_ref, sum_ref):
+def force_kernel(
+    pairs_ref, pos_ref, strength_ref, out_ref, x_ref, new_ref, partner_ref, own_ref, sum_ref
+):
     images, _, atoms = x_ref.shape
+    blocks, _, _, local_atoms = out_ref.shape
     tiles = atoms // TB
     row = lax.broadcasted_iota(jnp.int32, (ROWS, atoms), 0)
     one = jnp.ones((ROWS, atoms), jnp.float32)
@@ -30,7 +34,11 @@
     for pair in range(images // 2):
         partner_rows = []
         for side in range(2):
-            x = x_ref[2 * pair + side]
+            image = 2 * pair + side
+            x_ref[image] = zero
+            for part in range(3):
+                x_ref[image, part : part + 1] = pos_ref[part, image : image + 1]
+            x = x_ref[image]
             xh, xm, xl = three_parts(x)
             vh, vm, vl = three_parts(x * LOG2E)
             const = (-0.5 * LOG2E) * jnp.sum(x * x, axis=0, keepdims=True) + log_strength
@@ -81,63 +89,65 @@
             total = part[0:8] + part[8:16] + part[16:24]
             x = x_ref[2 * pair + side, :, lanes]
             force = x * total[3:4] - total
-            out_ref[2 * pair + side, :, lanes] = x + STEP_SIZE * force
+            new_ref[2 * pair + side, :, lanes] = x + STEP_SIZE * force
         return carry
 
-    lax.fori_loop(0, (images // 2) * tiles, step, 0)
+    lax.fori_loop(0, (images // 2) * tiles, step, 0, unroll=UNROLL)
+    for image in range(images):
+        for block in range(blocks):
+            for part in range(3):
+                out_ref[block, part, image : image + 1] = new_ref[
+                    image, part : part + 1, block * local_atoms : (block + 1) * local_atoms
+                ]
 
 
-def moved_images(x, strength, tile_pairs):
-    images, _, atoms = x.shape
+def moved_images(positions, strength, tile_pairs, blocks):
+    _, images, atoms = positions.shape
     tiles = atoms // TB
     pairs = images // 2
     vmem = pl.BlockSpec(memory_space=pltpu.VMEM)
     return pl.pallas_call(
         force_kernel,
-        out_shape=jax.ShapeDtypeStruct(x.shape, jnp.float32),
+        out_shape=jax.ShapeDtypeStruct((blocks, 3, images, atoms // blocks), jnp.float32),
         in_specs=[pl.BlockSpec(memory_space=pltpu.SMEM), vmem, vmem],
         out_specs=vmem,
         scratch_shapes=[
+            pltpu.VMEM((images, ROWS, atoms), jnp.float32),
+            pltpu.VMEM((images, ROWS, atoms), jnp.float32),
             pltpu.VMEM((pairs, tiles, TB, DEPTH), jnp.bfloat16),
             pltpu.VMEM((pairs, tiles, DEPTH, 2 * TB), jnp.bfloat16),
             pltpu.VMEM((pairs, tiles, 48, 2 * TB), jnp.bfloat16),
         ],
         name="force",
-    )(tile_pairs, x, strength[None, :])
+    )(tile_pairs, positions, strength[None, :])
 
 
 def shards(positions, strength, tile_pairs, source_segment):
-    count = positions.shape[1]
+    _, count, local_atoms = positions.shape
     blocks = lax.axis_size("atom")
-    mine = count // blocks
     images_total = count * lax.axis_size("img")
     own = lax.all_to_all(positions, "atom", split_axis=1, concat_axis=2, tiled=True)
-    x = jnp.pad(own.transpose(1, 0, 2), ((0, 0), (0, ROWS - 3), (0, 0)))
-    moved = moved_images(x, strength, tile_pairs)[:, :3]
-    everyone = images_total // mine
-    before = lax.ppermute(
-        moved[mine - 1 :], ("img", "atom"), [(i, i + 1) for i in range(everyone - 1)]
-    )
-    segments = moved - jnp.concatenate([before, moved[: mine - 1]], axis=0)
-    squares = jnp.sum(segments * segments, axis=(1, 2))
-    first = lax.axis_index(("img", "atom")) * mine
-    ids = first + jnp.arange(mine, dtype=jnp.int32)
-    own_lengths = jnp.where(ids >= 1, jnp.sqrt(1.0 + squares), 0.0)
-    lengths = lax.all_gather(own_lengths, ("img", "atom"), axis=0, tiled=True)
-    back = lax.all_to_all(moved.transpose(1, 0, 2), "atom", split_axis=2, concat_axis=1, tiled=True)
+    moved = moved_images(own, strength, tile_pairs, blocks)
+    back = lax.all_to_all(moved, "atom", split_axis=0, concat_axis=0, tiled=True)
+    back = back.transpose(1, 0, 2, 3).reshape(3, count, local_atoms)
     ends = lax.axis_size("img") - 1
     head = lax.ppermute(back[:, count - 1 :], "img", [(i, i + 1) for i in range(ends)])
     tail = lax.ppermute(back[:, :1], "img", [(i + 1, i) for i in range(ends)])
+    previous = jnp.concatenate([head, back[:, : count - 1]], axis=1)
+    following = jnp.concatenate([back[:, 1:], tail], axis=1)
     numbers = lax.axis_index("img") * count + jnp.arange(count, dtype=jnp.int32)
     columns = jnp.arange(images_total, dtype=jnp.int32)[None, :]
+    apart = back - previous
+    partial_squares = jnp.sum(apart * apart, axis=(0, 2))
+    spread = jnp.sum(jnp.where(columns == numbers[:, None], partial_squares[:, None], 0.0), axis=0)
+    squares = lax.psum(spread, ("img", "atom"))
+    lengths = jnp.where(columns[0] >= 1, jnp.sqrt(1.0 + squares), 0.0)
     segment = source_segment[:, None]
     arc_low = jnp.sum(jnp.where(columns < segment, lengths[None, :], 0.0), axis=1)
     span = jnp.sum(jnp.where(columns == segment, lengths[None, :], 0.0), axis=1)
     target = numbers.astype(jnp.float32) * (jnp.sum(lengths) / (images_total - 1))
     weight = ((target - arc_low) / span)[None, :, None]
     later = (source_segment > numbers)[None, :, None]
-    previous = jnp.concatenate([head, back[:, : count - 1]], axis=1)
-    following = jnp.concatenate([back[:, 1:], tail], axis=1)
     low = jnp.where(later, back, previous)
     high = jnp.where(later, following, back)
     return (1.0 - weight) * low + weight * high

time: 198 us -> 134 us (0.68)
  local copies, waits for them, and re-layouts: 36.4 us -> 4.54 us
  Pallas kernels: 75.4 us -> 48.1 us
  waiting for transfers between devices: 20.4 us -> 24.4 us
  other arithmetic: 5.17 us -> 1.97 us
  blocking collectives: 40.7 us -> 38.1 us
    unnamed x1 -> x0, blocking collectives: 40.7 us -> none
    psum x0 -> x1, blocking collectives: none -> 38.1 us  [shards(): squares = lax.psum(spread, ('img', 'atom'))]
    pallas_call x1, Pallas kernels: 75.4 us -> 48.1 us  [moved_images(): pl.pallas_call(force_kernel, out_shape=jax.ShapeDtypeStruct((blocks, 3, i...]
    unnamed x7 -> x6, local copies, waits for them, and re-layouts: 19.6 us -> 3.37 us
    all_to_all x1, waiting for transfers between devices: 0.01 us -> 10.6 us  [shards(): lax.all_to_all(moved, 'atom', split_axis=0, concat_axis=0, tiled=True)]
    all_to_all x2 -> x0, local copies, waits for them, and re-layouts: 6.89 us -> none  [shards(): lax.all_to_all(moved.transpose(1, 0, 2), 'atom', split_axis=2, concat_axi...]
    ppermute x1 -> x0, waiting for transfers between devices: 6 us -> none  [shards(): lax.ppermute(moved[mine - 1:], ('img', 'atom'), [(i, i + 1) for i in rang...]
    transpose x1 -> x0, local copies, waits for them, and re-layouts: 5.81 us -> none  [shards(): moved.transpose(1, 0, 2)]
  transfers between devices with their start and end apart: 5 -> 4, of which waited for: 3 -> 2; matrix products, arithmetic and copies ran while one was open for 2% -> 1% of each run, Pallas kernels for 0% -> 0%
where the time goes in v2:
time: 134 us; the launch traced here: 133 us
  Pallas kernels  48.1 us (36%)
  blocking collectives  38.1 us (28%)
  waiting for transfers between devices  24.4 us (18%)
  starting transfers between devices  14.9 us (11%)
  local copies, waits for them, and re-layouts  4.54 us (3%)
  other arithmetic  1.97 us (1%)
    pallas_call x1, Pallas kernels, moved_images(): pl.pallas_call(force_kernel, out_shape=jax.ShapeDtypeStruct((blocks, 3, i...  48.1 us
    psum x1, blocking collectives, shards(): squares = lax.psum(spread, ('img', 'atom'))  38.1 us
    all_to_all x1, waiting for transfers between devices, shards(): lax.all_to_all(positions, 'atom', split_axis=1, concat_axis=2, tiled=True)  13.8 us
    all_to_all x1, waiting for transfers between devices, shards(): lax.all_to_all(moved, 'atom', split_axis=0, concat_axis=0, tiled=True)  10.6 us
    all_to_all x1, starting transfers between devices, shards(): lax.all_to_all(positions, 'atom', split_axis=1, concat_axis=2, tiled=True)  5 us
    ppermute x1, starting transfers between devices, shards(): tail = lax.ppermute(back[:, :1], 'img', [(i + 1, i) for i in range(ends)])  4.54 us
    all_to_all x1, starting transfers between devices, shards(): lax.all_to_all(moved, 'atom', split_axis=0, concat_axis=0, tiled=True)  3.46 us
    unnamed x6, local copies, waits for them, and re-layouts  3.37 us
  transfers between devices with their start and end apart: 4, of which 2 were waited for; matrix products, arithmetic and copies ran while one was open for 1% of the time, Pallas kernels for 0%

profile of v2, /device:TPU:4, one launch (start us, length us, event | category | flops | bytes accessed | tf_op | source)
XLA Modules:
  0.0 132.7 jit_solution(13333128971401904265)
XLA Ops:
  0.0 2.1 %copy.14 = f32[3,32,1024]{2,0,1:T(4,128)} copy(f32[3,32,1024]{2,1,0:T(8,128)} %param.4) | data formatting | bytes 786432 | tf_op args[0]
  2.1 0.0 copy-start
  2.1 5.0 %all-to-all-start = ((f32[3,32,1024]{2,0,1:T(4,128)}), f32[3,32,1024]{2,0,1:T(4,128)S(1)}, u32[]{:S(2)}, u32[]{:S(2)}) async-start(f32[3,32,1024]{2,0,1:T(4,128)} %copy.14), calls=%async_computation | async-start | bytes 1048576 | tf_op jit(solution)/shard_map/all_to_all | solution.py:129
  7.1 0.0 copy-done
  7.1 0.7 copy.16.pairs_ref
  7.7 13.8 %all-to-all-done = f32[3,32,1024]{2,0,1:T(4,128)S(1)} async-done(((f32[3,32,1024]{2,0,1:T(4,128)}), f32[3,32,1024]{2,0,1:T(4,128)S(1)}, u32[]{:S(2)}, u32[]{:S(2)}) %all-to-all-start) | async-done | bytes 393248 | tf_op jit(solution)/shard_map/all_to_all | solution.py:129
  21.6 1.0 copy.15
  22.5 48.1 %force.1 = f32[4,3,8,1024]{3,2,1,0:T(8,128)} custom-call(s32[32,8]{1,0:T(8,128)} %copy.16.pairs_ref, f32[3,8,4096]{2,1,0:T(8,128)} %bitcast.19, f32[1,4096]{1,0:T(1,128)} %bitcast.20), custom_call_target="tpu_custom_call" | custom-call | tf_op jit(solution)/shard_map/force/pallas_call | solution.py:109
  70.6 3.5 %all-to-all-start.1 = ((f32[4,3,8,1024]{3,2,1,0:T(8,128)}), f32[4,3,8,1024]{3,2,1,0:T(8,128)S(1)}, u32[]{:S(2)}, u32[]{:S(2)}) async-start(f32[4,3,8,1024]{3,2,1,0:T(8,128)} %force.1), calls=%async_computation.1 | async-start | bytes 786432 | tf_op jit(solution)/shard_map/all_to_all | solution.py:131
  74.1 0.0 copy-start.1
  74.1 0.6 copy-done.1
  74.8 10.6 %all-to-all-done.1 = f32[4,3,8,1024]{3,2,1,0:T(8,128)S(1)} async-done(((f32[4,3,8,1024]{3,2,1,0:T(8,128)}), f32[4,3,8,1024]{3,2,1,0:T(8,128)S(1)}, u32[]{:S(2)}, u32[]{:S(2)}) %all-to-all-start.1) | async-done | bytes 393248 | tf_op jit(solution)/shard_map/all_to_all | solution.py:131
  85.4 1.9 %collective-permute-start = (f32[3,1,1024]{2,1,0:T(1,128)S(1)}, f32[3,1,1024]{2,1,0:T(1,128)S(1)}, u32[]{:S(2)}, u32[]{:S(2)}) collective-permute-start(f32[3,1,1024]{2,1,0:T(1,128)S(1)} %get-tuple-element.9), channel_id=1, source_target_pairs={{0,4},{4,8},{8,12},{12,16},{16,20},{20,24},{24,28},{1,5},{5,9},{9,... | collective-permute-start | bytes 36872 | tf_op jit(solution)/shard_map/ppermute | solution.py:134
  87.3 0.1 fusion.8
  87.4 4.5 %collective-permute-start.1 = (f32[3,1,1024]{2,1,0:T(1,128)S(1)}, f32[3,1,1024]{2,1,0:T(1,128)S(1)}, u32[]{:S(2)}, u32[]{:S(2)}) collective-permute-start(f32[3,1,1024]{2,1,0:T(1,128)S(1)} %get-tuple-element.10), channel_id=1, source_target_pairs={{4,0},{8,4},{12,8},{16,12},{20,16},{24,20},{28,24},{5,1},{9,5},{13... | collective-permute-start | bytes 36872 | tf_op jit(solution)/shard_map/ppermute | solution.py:135
  91.9 0.0 collective-permute-done
  92.0 0.2 fusion.3
  92.1 0.1 broadcast_in_dim.55
  92.2 0.1 select_reduce_fusion.2
  92.3 38.1 %psum.7 = f32[256]{0:T(256)S(1)} all-reduce(f32[256]{0:T(256)S(1)} %select_reduce_fusion.2), channel_id=1, replica_groups=mesh['img'=8,'atom'=4] {'img','atom'}, use_global_device_ids=true, to_apply=%region_2.3 | all-reduce | flops 256 | bytes 2048 | tf_op jit(solution)/shard_map/psum | solution.py:143
  130.4 0.6 fusion.6
  131.0 0.2 select_reduce_fusion.1
  131.8 0.0 collective-permute-done.1
  131.8 0.9 fusion.1
  (5 shorter events, 0.1 us)
Async XLA Ops:
  2.1 5.0 %copy-start = (s32[32,8]{0,1:T(8,128)S(1)}, s32[32,8]{0,1:T(8,128)}, u32[]{:S(2)}) copy-start(s32[32,8]{0,1:T(8,128)} %param.6) | copy-start | bytes 3076
  2.1 19.5 %all-to-all-start = ((f32[3,32,1024]{2,0,1:T(4,128)}), f32[3,32,1024]{2,0,1:T(4,128)S(1)}, u32[]{:S(2)}, u32[]{:S(2)}) async-start(f32[3,32,1024]{2,0,1:T(4,128)} %copy.14), calls=%async_computation | async-start | bytes 1048576 | tf_op jit(solution)/shard_map/all_to_all | solution.py:129
  70.6 14.7 %all-to-all-start.1 = ((f32[4,3,8,1024]{3,2,1,0:T(8,128)}), f32[4,3,8,1024]{3,2,1,0:T(8,128)S(1)}, u32[]{:S(2)}, u32[]{:S(2)}) async-start(f32[4,3,8,1024]{3,2,1,0:T(8,128)} %force.1), calls=%async_computation.1 | async-start | bytes 786432 | tf_op jit(solution)/shard_map/all_to_all | solution.py:131
  74.1 0.7 copy-start.1
  85.4 6.5 %collective-permute-start = (f32[3,1,1024]{2,1,0:T(1,128)S(1)}, f32[3,1,1024]{2,1,0:T(1,128)S(1)}, u32[]{:S(2)}, u32[]{:S(2)}) collective-permute-start(f32[3,1,1024]{2,1,0:T(1,128)S(1)} %get-tuple-element.9), channel_id=1, source_target_pairs={{0,4},{4,8},{8,12},{12,16},{16,20},{20,24},{24,28},{1,5},{5,9},{9,... | collective-permute-start | bytes 36872 | tf_op jit(solution)/shard_map/ppermute | solution.py:134
  87.4 44.4 %collective-permute-start.1 = (f32[3,1,1024]{2,1,0:T(1,128)S(1)}, f32[3,1,1024]{2,1,0:T(1,128)S(1)}, u32[]{:S(2)}, u32[]{:S(2)}) collective-permute-start(f32[3,1,1024]{2,1,0:T(1,128)S(1)} %get-tuple-element.10), channel_id=1, source_target_pairs={{4,0},{8,4},{12,8},{16,12},{20,16},{24,20},{28,24},{5,1},{9,5},{13... | collective-permute-start | bytes 36872 | tf_op jit(solution)/shard_map/ppermute | solution.py:135
